TPU v7x, 32 devices: a whole 2x2x4 slice. The times are simulated.
32 devices in a mesh: groups: 1, blk: 16 (over z, y, x), head: 2 (over core).
Axes of the slice: x: 2, y: 2, z: 4, core: 2. Of those that a mesh axis runs over, the one named last changes fastest.
Arguments:
- queries: bfloat16 [128, 8192], P(('groups', 'blk'), 'head'), may hold values from -6 to 6
- key_cache: bfloat16 [2, 32768, 8, 128], P('groups', 'blk', 'head'), may hold values from -18 to 18
- value_cache: bfloat16 [2, 32768, 8, 128], P('groups', 'blk', 'head'), may hold values from -6 to 6
- lengths: int32 [2], P('groups'), may hold values from 0 to 32704
- residual: bfloat16 [128, 8192], P('groups', 'blk'), may hold values from -6 to 6
- out_weight: bfloat16 [8192, 8192], P('head', 'blk'), may hold values from -0.0625 to 0.0625
- norm_gain: bfloat16 [8192], P('blk'), may hold values from 0.099609375 to 1.8984375
- gate_weight: bfloat16 [8192, 16384], P(None, ('head', 'blk')), may hold values from -0.0625 to 0.0625
- up_weight: bfloat16 [8192, 16384], P(None, ('head', 'blk')), may hold values from -0.0625 to 0.0625
- down_weight: bfloat16 [16384, 8192], P('head', 'blk'), may hold values from -0.046875 to 0.046875
Outputs:
- layer_out: bfloat16 [128, 8192], P('groups', 'blk')
Inputs may be any that keep to these rules, and one draw needn't show every extreme that they name: lengths[b] + 64 <= 32768; the cache holds sequence b's new keys and values at positions lengths[b] to lengths[b] + 63.
All inputs are finite; a program needn't handle non-finite values.
Results may differ from a plain program's by a relative error of at most 0.01.
Values may be sent and summed in bfloat16 or wider, within the bound.
No kernel may reach another device: no remote copies, remote signals or barrier semaphores. Data moves between devices by JAX's collectives and lax.ppermute only.
A program may use at most 128 MiB of HBM per device.

v0:
```python
import jax
import jax.numpy as jnp
from jax import lax
from jax.sharding import PartitionSpec as P

D = 8192
neg_big = -1e30
epsilon = 1e-06


def body(
    queries,
    key_cache,
    value_cache,
    lengths,
    residual,
    out_weight,
    norm_gain,
    gate_weight,
    up_weight,
    down_weight,
):
    blocks = lax.axis_size("blk")
    my_block = lax.axis_index("blk")
    batch, ctx_dev, kv_local, head_dim = key_cache.shape
    rows_dev = queries.shape[0]
    rows_all = rows_dev * blocks
    new_tokens = rows_all // batch
    heads_local = queries.shape[1] // head_dim
    group_size = heads_local // kv_local
    all_queries = lax.all_gather(queries, "blk", axis=0, tiled=True)
    shaped = all_queries.reshape(batch, new_tokens, kv_local, group_size, head_dim)
    scores = jnp.einsum(
        "bqkgd,bckd->bqkgc", shaped, key_cache, preferred_element_type=jnp.float32
    ) * head_dim ** (-0.5)
    query_pos = lengths[:, None] + jnp.arange(new_tokens, dtype=jnp.int32)[None, :]
    key_pos = my_block * ctx_dev + jnp.arange(ctx_dev, dtype=jnp.int32)
    visible = key_pos[None, None, None, None, :] <= query_pos[:, :, None, None, None]
    block_max = jnp.max(jnp.where(visible, scores, neg_big), axis=-1)
    weights = jnp.where(visible, jnp.exp(scores - block_max[..., None]), 0.0)
    block_sum = jnp.sum(weights, axis=-1)
    block_out = jnp.einsum(
        "bqkgc,bckd->bqkgd",
        weights.astype(jnp.bfloat16),
        value_cache,
        preferred_element_type=jnp.float32,
    )
    block_mean = (block_out / jnp.maximum(block_sum, 1.0)[..., None]).astype(jnp.bfloat16)
    row_max = block_max.reshape(rows_all, heads_local)
    row_sum = block_sum.reshape(rows_all, heads_local)
    row_mean = block_mean.reshape(rows_all, heads_local, head_dim)
    got_max, got_sum = (
        lax.all_to_all(row_max[None], "blk", split_axis=1, concat_axis=0, tiled=True),
        lax.all_to_all(row_sum[None], "blk", split_axis=1, concat_axis=0, tiled=True),
    )
    got_mean = lax.all_to_all(row_mean[None], "blk", split_axis=1, concat_axis=0, tiled=True)
    top = jnp.max(got_max, axis=0)
    factor = got_sum * jnp.exp(got_max - top[None])
    total_sum = jnp.sum(factor, axis=0)
    total_out = jnp.sum(got_mean.astype(jnp.float32) * factor[..., None], axis=0)
    attn = (
        (total_out / total_sum[..., None])
        .astype(jnp.bfloat16)
        .reshape(rows_dev, heads_local * head_dim)
    )
    proj_part = jnp.dot(
        lax.all_gather(attn, "blk", axis=0, tiled=True),
        out_weight,
        preferred_element_type=jnp.float32,
    )
    projected = lax.psum(proj_part.astype(jnp.bfloat16), "head").astype(jnp.float32)
    stream = residual.astype(jnp.float32) + projected
    squares = lax.psum(jnp.sum(stream * stream, axis=1), "blk")
    normed = (
        stream * lax.rsqrt(squares / D + epsilon)[:, None] * norm_gain.astype(jnp.float32)[None, :]
    ).astype(jnp.bfloat16)
    piece = lax.all_gather(normed, "blk", axis=1, tiled=True)
    gate = jnp.dot(piece, gate_weight, preferred_element_type=jnp.float32)
    up = jnp.dot(piece, up_weight, preferred_element_type=jnp.float32)
    hidden = (jax.nn.silu(gate) * up).astype(jnp.bfloat16)
    down_part = jnp.dot(
        lax.all_gather(hidden, "blk", axis=1, tiled=True),
        down_weight,
        preferred_element_type=jnp.float32,
    )
    down_total = lax.psum(down_part.astype(jnp.bfloat16), "head").astype(jnp.float32)
    return (stream + down_total).astype(jnp.bfloat16)


def solution(mesh):
    in_specs = (
        P(("groups", "blk"), "head"),
        P("groups", "blk", "head", None),
        P("groups", "blk", "head", None),
        P("groups"),
        P("groups", "blk"),
        P("head", "blk"),
        P("blk"),
        P(None, ("head", "blk")),
        P(None, ("head", "blk")),
        P("head", "blk"),
    )
    out_specs = P("groups", "blk")
    return jax.shard_map(body, mesh=mesh, in_specs=in_specs, out_specs=out_specs, check_vma=False)
```

profile of v0, /device:TPU:0, one launch (start us, length us, event | category | flops | bytes accessed | tf_op | source)
XLA Modules:
  0.0 444.1 jit_solution(5362369163561286765)
XLA Ops:
  6.5 0.7 all-gather.5.cloned.1.call-update
  7.3 0.7 iota_add_fusion.1
  8.2 59.7 %all-gather.5.cloned.1.call-done = bf16[128,4096]{1,0:T(8,128)(2,1)} async-done(((bf16[8,4096]{1,0:T(8,128)(2,1)}), bf16[128,4096]{1,0:T(8,128)(2,1)}) %all-gather.5.cloned.1.call-update) | async-done | bytes 1048592 | tf_op jit(solution)/shard_map/all_gather | solution.py:31
  67.9 1.5 copy.45
  69.4 17.1 %fusion = (f32[2,64,4,8]{1,3,2,0:T(8,128)S(1)}, f32[2,4,2048,64,8]{2,3,4,1,0:T(8,128)}) fusion(pred[2,64,2048]{2,1,0:T(8,128)(4,1)S(1)} %broadcast_compare_fusion, bf16[2,64,4,8,128]{4,3,2,1,0:T(8,128)(2,1)S(1)} %bitcast.53, bf16[2,2048,4,128,1]{3,2,1,0,4:T(4,128)(2,1)} %bitcast.55), kind=kOutput, calls=%fused_computation.2 | convolution fusion | flops 2172645376 | bytes 39075840 | tf_op jit(solution)/shard_map/bqkgd,bckd->bqkgc/dot_general | solution.py:33
  86.5 15.1 %fusion.3 = f32[2,64,4,8]{1,3,2,0:T(8,128)S(1)} fusion(f32[2,4,2048,64,8]{2,3,4,1,0:T(8,128)} %get-tuple-element.8, f32[2,64,4,8]{1,3,2,0:T(8,128)S(1)} %get-tuple-element.7, pred[2,64,2048]{2,1,0:T(8,128)(4,1)S(1)} %broadcast_compare_fusion), kind=kLoop, calls=%fused_computation.5 | loop fusion | flops 33550336 | bytes 33849344 | tf_op jit(solution)/shard_map/reduce_sum | solution.py:41
  102.3 0.8 reduce.2
  103.1 0.7 reshape.82
  103.8 4.4 %all-to-all-start.2 = ((f32[16,1,256]{2,1,0:T(1,128)}), f32[16,1,256]{2,1,0:T(1,128)S(1)}, u32[]{:S(2)}, u32[]{:S(2)}) async-start(f32[16,1,256]{2,1,0:T(1,128)} %reshape.82), calls=%async_computation.2 | async-start | bytes 32768 | tf_op jit(solution)/shard_map/all_to_all | solution.py:53
  108.5 0.8 reduce
  109.3 0.7 reshape.80
  110.0 5.6 %all-to-all-done.2 = f32[16,1,256]{2,1,0:T(1,128)S(1)} async-done(((f32[16,1,256]{2,1,0:T(1,128)}), f32[16,1,256]{2,1,0:T(1,128)S(1)}, u32[]{:S(2)}, u32[]{:S(2)}) %all-to-all-start.2) | async-done | bytes 16416 | tf_op jit(solution)/shard_map/all_to_all | solution.py:53
  115.6 3.5 all-to-all-start.1
  119.1 15.6 %fusion.12 = bf16[2,64,4,8,128]{4,1,3,2,0:T(8,128)(2,1)S(1)} fusion(bf16[2,2048,4,128,1]{3,2,1,0,4:T(4,128)(2,1)} %bitcast.63, f32[2,4,2048,64,8]{2,3,4,1,0:T(8,128)} %get-tuple-element.8, f32[2,64,4,8]{1,3,2,0:T(8,128)S(1)} %get-tuple-element.7, pred[2,64,2048]{2,1,0:T(8,128)(4,1)S(1)} %broadcast_compare_fusion, f32[2,64,4,8]{1,3,2,0:T(8,128)S(1)} %broadcast_maximum_fusion), kind=kOutput, calls=%fused_computation.15 | convolution fusion | flops 2182086656 | bytes 39092224 | tf_op jit(solution)/shard_map/bqkgc,bckd->bqkgd/dot_general | solution.py:42
  134.8 1.7 copy.33
  136.4 6.9 %all-to-all-start = ((bf16[1,128,32,128]{3,2,0,1:T(8,128)(2,1)}), bf16[1,128,32,128]{3,2,0,1:T(8,128)(2,1)S(1)}, u32[]{:S(2)}, u32[]{:S(2)}) async-start(bf16[1,128,32,128]{3,2,0,1:T(8,128)(2,1)} %bitcast.5), calls=%async_computation | async-start | bytes 2097152 | tf_op jit(solution)/shard_map/all_to_all | solution.py:56
  145.2 19.7 %all-to-all-done = bf16[1,128,32,128]{3,2,0,1:T(8,128)(2,1)S(1)} async-done(((bf16[1,128,32,128]{3,2,0,1:T(8,128)(2,1)}), bf16[1,128,32,128]{3,2,0,1:T(8,128)(2,1)S(1)}, u32[]{:S(2)}, u32[]{:S(2)}) %all-to-all-start) | async-done | bytes 1048608 | tf_op jit(solution)/shard_map/all_to_all | solution.py:56
  164.9 0.7 fusion.11
  165.8 0.7 copy.60
  166.5 54.4 %all-gather.7.cloned.1.call-done = bf16[128,4096]{1,0:T(8,128)(2,1)} async-done(((bf16[8,4096]{1,0:T(8,128)(2,1)}), bf16[128,4096]{1,0:T(8,128)(2,1)}) %all-gather.7.cloned.1.call-update) | async-done | bytes 1048592 | tf_op jit(solution)/shard_map/all_gather | solution.py:67
  220.9 3.9 convolution_convert_fusion
  224.9 16.8 %all-reduce.3.cloned.1.call-done = bf16[128,512]{1,0:T(8,128)(2,1)} async-done(((bf16[128,512]{1,0:T(8,128)(2,1)}), bf16[128,512]{1,0:T(8,128)(2,1)}) %all-reduce.3.cloned.1.call-update) | async-done | bytes 131088 | tf_op jit(solution)/shard_map/psum | solution.py:71
  241.7 1.0 multiply_reduce_fusion
  242.7 42.0 %psum.22 = f32[128]{0:T(128)S(1)} all-reduce(f32[128]{0:T(128)S(1)} %multiply_reduce_fusion), channel_id=1, replica_groups=mesh['groups'=1,'blk'=16,'head'=2] {'blk'}, use_global_device_ids=true, to_apply=%region_7.8 | all-reduce | flops 128 | bytes 1024 | tf_op jit(solution)/shard_map/psum | solution.py:73
  284.7 1.7 multiply_convert_fusion
  286.5 56.9 %all-gather.9.cloned.1.call-done = bf16[128,8192]{1,0:T(8,128)(2,1)} async-done(((bf16[128,512]{1,0:T(8,128)(2,1)}), bf16[128,8192]{1,0:T(8,128)(2,1)}) %all-gather.9.cloned.1.call-update) | async-done | bytes 2097168 | tf_op jit(solution)/shard_map/all_gather | solution.py:77
  343.3 5.4 %fusion.23 = f32[128,512]{1,0:T(8,128)S(1)} fusion(bf16[128,8192]{1,0:T(8,128)(2,1)} %all-gather.9.cloned.1.call-done, bf16[8192,512]{1,0:T(8,128)(2,1)} %param.17), kind=kOutput, calls=%fused_computation.37 | convolution fusion | flops 1073741824 | bytes 10747904 | tf_op jit(solution)/shard_map/dot_general | solution.py:78
  348.7 5.4 %fusion.17 = bf16[128,512]{1,0:T(8,128)(2,1)} fusion(bf16[128,8192]{1,0:T(8,128)(2,1)S(1)} %copy-done, bf16[8192,512]{1,0:T(8,128)(2,1)} %param.18, f32[128,512]{1,0:T(8,128)S(1)} %fusion.23), kind=kOutput, calls=%fused_computation.17 | convolution fusion | flops 1074135040 | bytes 10878976 | tf_op jit(solution)/shard_map/dot_general | solution.py:79
  354.3 59.2 %all-gather.11.cloned.1.call-done = bf16[128,8192]{1,0:T(8,128)(2,1)} async-done(((bf16[128,512]{1,0:T(8,128)(2,1)}), bf16[128,8192]{1,0:T(8,128)(2,1)}) %all-gather.11.cloned.1.call-update) | async-done | bytes 2097168 | tf_op jit(solution)/shard_map/all_gather | solution.py:82
  413.4 5.9 %convolution_convert_fusion.1 = bf16[128,512]{1,0:T(8,128)(2,1)} fusion(bf16[128,8192]{1,0:T(8,128)(2,1)} %all-gather.11.cloned.1.call-done, bf16[8192,512]{1,0:T(8,128)(2,1)} %param.19), kind=kOutput, calls=%fused_computation.19 | convolution fusion | flops 1073807360 | bytes 10616832 | tf_op jit(solution)/shard_map/dot_general | solution.py:81
  419.4 16.2 %all-reduce.5.cloned.1.call-done = bf16[128,512]{1,0:T(8,128)(2,1)} async-done(((bf16[128,512]{1,0:T(8,128)(2,1)}), bf16[128,512]{1,0:T(8,128)(2,1)}) %all-reduce.5.cloned.1.call-update) | async-done | bytes 131088 | tf_op jit(solution)/shard_map/psum | solution.py:86
  435.6 1.6 add_convert_fusion
  (39 shorter events, 3.4 us)
Async XLA Ops:
  6.5 61.4 %all-gather.5.cloned.1.call-start = ((), (), s32[]{:S(2)}) async-start(), calls=%async_computation.3 | async-start | bytes 1114112 | tf_op jit(solution)/shard_map/all_gather | solution.py:31
  103.8 11.8 %all-to-all-start.2 = ((f32[16,1,256]{2,1,0:T(1,128)}), f32[16,1,256]{2,1,0:T(1,128)S(1)}, u32[]{:S(2)}, u32[]{:S(2)}) async-start(f32[16,1,256]{2,1,0:T(1,128)} %reshape.82), calls=%async_computation.2 | async-start | bytes 32768 | tf_op jit(solution)/shard_map/all_to_all | solution.py:53
  115.6 20.8 %all-to-all-start.1 = ((f32[16,1,256]{2,1,0:T(1,128)}), f32[16,1,256]{2,1,0:T(1,128)S(1)}, u32[]{:S(2)}, u32[]{:S(2)}) async-start(f32[16,1,256]{2,1,0:T(1,128)} %reshape.80), calls=%async_computation.1 | async-start | bytes 32768 | tf_op jit(solution)/shard_map/all_to_all | solution.py:54
  134.7 90.1 %copy-start.3 = (bf16[512]{0:T(512)(128)(2,1)S(1)}, bf16[512]{0:T(512)(128)(2,1)}, u32[]{:S(2)}) copy-start(bf16[512]{0:T(512)(128)(2,1)} %param.16) | copy-start | bytes 3076
  134.7 106.9 %copy-start.1 = (bf16[128,512]{1,0:T(8,128)(2,1)S(1)}, bf16[128,512]{1,0:T(8,128)(2,1)}, u32[]{:S(2)}) copy-start(bf16[128,512]{1,0:T(8,128)(2,1)} %param.14) | copy-start | bytes 393220
  136.4 28.5 %all-to-all-start = ((bf16[1,128,32,128]{3,2,0,1:T(8,128)(2,1)}), bf16[1,128,32,128]{3,2,0,1:T(8,128)(2,1)S(1)}, u32[]{:S(2)}, u32[]{:S(2)}) async-start(bf16[1,128,32,128]{3,2,0,1:T(8,128)(2,1)} %bitcast.5), calls=%async_computation | async-start | bytes 2097152 | tf_op jit(solution)/shard_map/all_to_all | solution.py:56
  143.3 77.6 %all-gather.7.cloned.1.call-start = ((), (), s32[]{:S(2)}) async-start(), calls=%async_computation.4 | async-start | bytes 1114112 | tf_op jit(solution)/shard_map/all_gather | solution.py:67
  166.4 75.2 %all-reduce.3.cloned.1.call-start = ((), (), s32[]{:S(2)}) async-start(), calls=%async_computation.5 | async-start | bytes 262144 | tf_op jit(solution)/shard_map/psum | solution.py:71
  224.8 118.5 %all-gather.9.cloned.1.call-start = ((), (), s32[]{:S(2)}) async-start(), calls=%async_computation.6 | async-start | bytes 2228224 | tf_op jit(solution)/shard_map/all_gather | solution.py:77
  286.4 127.0 %all-gather.11.cloned.1.call-start = ((), (), s32[]{:S(2)}) async-start(), calls=%async_computation.7 | async-start | bytes 2228224 | tf_op jit(solution)/shard_map/all_gather | solution.py:82
  343.3 5.4 %copy-start = (bf16[128,8192]{1,0:T(8,128)(2,1)S(1)}, bf16[128,8192]{1,0:T(8,128)(2,1)}, u32[]{:S(2)}) copy-start(bf16[128,8192]{1,0:T(8,128)(2,1)} %all-gather.9.cloned.1.call-done) | copy-start | bytes 6291460
  354.2 81.4 %copy-start.2 = (bf16[128,512]{1,0:T(8,128)(2,1)S(1)}, bf16[128,512]{1,0:T(8,128)(2,1)}, u32[]{:S(2)}) copy-start(bf16[128,512]{1,0:T(8,128)(2,1)} %all-reduce.3.cloned.1.call-done) | copy-start | bytes 393220
  354.2 81.4 %all-reduce.5.cloned.1.call-start = ((), (), s32[]{:S(2)}) async-start(), calls=%async_computation.8 | async-start | bytes 262144 | tf_op jit(solution)/shard_map/psum | solution.py:86
Sparse Core Ops, SparseCore 0:
  10.1 57.7 all-gather.4
  166.6 54.2 all-gather.6
  224.9 16.7 all-reduce.2
  286.5 56.7 all-gather.8
  354.3 59.0 all-gather.10
  419.5 16.0 all-reduce.4
where the time goes:
time: 445 us; the launch traced here: 444 us
  waiting for transfers between devices  289 us (65%)
  matrix products  53.4 us (12%)
  blocking collectives  42 us (9%)
  other arithmetic  24 us (5%)
  starting transfers between devices  15.2 us (3%)
  between operations  13.7 us (3%)
  local copies, waits for them, and re-layouts  6.46 us (1%)
    all_gather x1, waiting for transfers between devices, body(): all_queries = lax.all_gather(queries, 'blk', axis=0, tiled=True)  59.7 us
    all_gather x1, waiting for transfers between devices, body(): lax.all_gather(hidden, 'blk', axis=1, tiled=True)  59.2 us
    all_gather x1, waiting for transfers between devices, body(): piece = lax.all_gather(normed, 'blk', axis=1, tiled=True)  56.9 us
    all_gather x1, waiting for transfers between devices, body(): lax.all_gather(attn, 'blk', axis=0, tiled=True)  54.4 us
    psum x1, blocking collectives, body(): squares = lax.psum(jnp.sum(stream * stream, axis=1), 'blk')  42 us
    all_to_all x1, waiting for transfers between devices, body(): lax.all_to_all(row_mean[None], 'blk', split_axis=1, concat_axis=0, tiled=...  19.7 us
    dot_general x1, matrix products, body(): jnp.einsum('bqkgd,bckd->bqkgc', shaped, key_cache, preferred_element_type...  17.1 us
    psum x1, waiting for transfers between devices, body(): lax.psum(proj_part.astype(jnp.bfloat16), 'head').astype(jnp.float32)  16.8 us
  transfers between devices with their start and end apart: 9, of which 8 were waited for; matrix products, arithmetic and copies ran while one was open for 5% of the time, Pallas kernels for 0%

commit v1 on v0

--- a/solution.py
+++ b/solution.py
@@ -6,6 +6,18 @@
 D = 8192
 neg_big = -1e30
 epsilon = 1e-06
+
+
+def ring_gather(value, axis, dim):
+    ways, here, step = (lax.axis_size(axis), lax.axis_index(axis), value.shape[dim])
+    dims = [n * ways if d == dim else n for d, n in enumerate(value.shape)]
+    full = lax.dynamic_update_slice_in_dim(
+        jnp.zeros(dims, value.dtype), value, here * step, axis=dim
+    )
+    for far in range(1, ways):
+        value = lax.ppermute(value, axis, [(d, (d + 1) % ways) for d in range(ways)])
+        full = lax.dynamic_update_slice_in_dim(full, value, (here - far) % ways * step, axis=dim)
+    return full
 
 
 def body(
@@ -79,9 +91,7 @@
     up = jnp.dot(piece, up_weight, preferred_element_type=jnp.float32)
     hidden = (jax.nn.silu(gate) * up).astype(jnp.bfloat16)
     down_part = jnp.dot(
-        lax.all_gather(hidden, "blk", axis=1, tiled=True),
-        down_weight,
-        preferred_element_type=jnp.float32,
+        ring_gather(hidden, "blk", 1), down_weight, preferred_element_type=jnp.float32
     )
     down_total = lax.psum(down_part.astype(jnp.bfloat16), "head").astype(jnp.float32)
     return (stream + down_total).astype(jnp.bfloat16)

time: 445 us -> 515 us (1.16)
  waiting for transfers between devices: 289 us -> 359 us
    ppermute x0 -> x15, waiting for transfers between devices: none -> 131 us  [ring_gather(): lax.ppermute(value, axis, [(d, (d + 1) % ways) for d in range(ways)])]
    all_gather x1 -> x0, waiting for transfers between devices: 59.2 us -> none  [body(): lax.all_gather(hidden, 'blk', axis=1, tiled=True)]
    all_to_all x1, waiting for transfers between devices: 0.01 us -> 5.69 us  [body(): lax.all_to_all(row_sum[None], 'blk', split_axis=1, concat_axis=0, tiled=T...]
    all_to_all x1, waiting for transfers between devices: 5.62 us -> 0.01 us  [body(): lax.all_to_all(row_max[None], 'blk', split_axis=1, concat_axis=0, tiled=T...]
  transfers between devices with their start and end apart: 9 -> 23, of which waited for: 8 -> 22; matrix products, arithmetic and copies ran while one was open for 5% -> 4% of each run, Pallas kernels for 0% -> 0%
where the time goes in v1:
time: 515 us
  waiting for transfers between devices  359 us (70%)
  matrix products  52 us (10%)
  blocking collectives  42 us (8%)
  other arithmetic  23.8 us (5%)
  starting transfers between devices  16.5 us (3%)
  between operations  13.5 us (3%)
  local copies, waits for them, and re-layouts  8.16 us (2%)
    ppermute x15, waiting for transfers between devices, ring_gather(): lax.ppermute(value, axis, [(d, (d + 1) % ways) for d in range(ways)])  131 us
    all_gather x1, waiting for transfers between devices, body(): all_queries = lax.all_gather(queries, 'blk', axis=0, tiled=True)  59.7 us
    all_gather x1, waiting for transfers between devices, body(): piece = lax.all_gather(normed, 'blk', axis=1, tiled=True)  56.9 us
    all_gather x1, waiting for transfers between devices, body(): lax.all_gather(attn, 'blk', axis=0, tiled=True)  54.4 us
    psum x1, blocking collectives, body(): squares = lax.psum(jnp.sum(stream * stream, axis=1), 'blk')  42 us
    all_to_all x1, waiting for transfers between devices, body(): lax.all_to_all(row_mean[None], 'blk', split_axis=1, concat_axis=0, tiled=...  19.9 us
    dot_general x1, matrix products, body(): jnp.einsum('bqkgd,bckd->bqkgc', shaped, key_cache, preferred_element_type...  17 us
    psum x1, waiting for transfers between devices, body(): lax.psum(proj_part.astype(jnp.bfloat16), 'head').astype(jnp.float32)  16.8 us
  transfers between devices with their start and end apart: 23, of which 22 were waited for; matrix products, arithmetic and copies ran while one was open for 4% of the time, Pallas kernels for 0%

profile of v1, /device:TPU:0, one launch (start us, length us, event | category | flops | bytes accessed | tf_op | source)
XLA Modules:
  0.0 514.5 jit_solution(9516726240578166572)
XLA Ops:
  8.2 59.7 %all-gather.4.cloned.1.call-done = bf16[128,4096]{1,0:T(8,128)(2,1)} async-done(((bf16[8,4096]{1,0:T(8,128)(2,1)}), bf16[128,4096]{1,0:T(8,128)(2,1)}) %all-gather.4.cloned.1.call-update) | async-done | bytes 1048592 | tf_op jit(solution)/shard_map/all_gather | solution.py:43
  69.4 17.0 %fusion = (f32[2,64,4,8]{1,3,2,0:T(8,128)S(1)}, f32[2,4,2048,64,8]{2,3,4,1,0:T(8,128)}) fusion(pred[2,64,2048]{2,1,0:T(8,128)(4,1)S(1)} %broadcast_compare_fusion, bf16[2,64,4,8,128]{4,3,2,1,0:T(8,128)(2,1)S(1)} %bitcast.53, bf16[2,2048,4,128,1]{3,2,1,0,4:T(4,128)(2,1)} %bitcast.55), kind=kOutput, calls=%fused_computation.2 | convolution fusion | flops 2172645376 | bytes 39075840 | tf_op jit(solution)/shard_map/bqkgd,bckd->bqkgc/dot_general | solution.py:45
  86.4 15.1 %fusion.3 = f32[2,64,4,8]{1,3,2,0:T(8,128)S(1)} fusion(f32[2,4,2048,64,8]{2,3,4,1,0:T(8,128)} %get-tuple-element.8, f32[2,64,4,8]{1,3,2,0:T(8,128)S(1)} %get-tuple-element.7, pred[2,64,2048]{2,1,0:T(8,128)(4,1)S(1)} %broadcast_compare_fusion), kind=kLoop, calls=%fused_computation.5 | loop fusion | flops 33550336 | bytes 33849344 | tf_op jit(solution)/shard_map/reduce_sum | solution.py:53
  103.6 4.5 all-to-all-start.1
  109.8 5.7 %all-to-all-done.1 = f32[16,1,256]{2,1,0:T(1,128)S(1)} async-done(((f32[16,1,256]{2,1,0:T(1,128)}), f32[16,1,256]{2,1,0:T(1,128)S(1)}, u32[]{:S(2)}, u32[]{:S(2)}) %all-to-all-start.1) | async-done | bytes 16416 | tf_op jit(solution)/shard_map/all_to_all | solution.py:66
  118.9 15.6 %fusion.12 = bf16[2,64,4,8,128]{4,1,3,2,0:T(8,128)(2,1)S(1)} fusion(bf16[2,2048,4,128,1]{3,2,1,0,4:T(4,128)(2,1)} %bitcast.63, f32[2,4,2048,64,8]{2,3,4,1,0:T(8,128)} %get-tuple-element.8, f32[2,64,4,8]{1,3,2,0:T(8,128)S(1)} %get-tuple-element.7, pred[2,64,2048]{2,1,0:T(8,128)(4,1)S(1)} %broadcast_compare_fusion, f32[2,64,4,8]{1,3,2,0:T(8,128)S(1)} %broadcast_maximum_fusion), kind=kOutput, calls=%fused_computation.15 | convolution fusion | flops 2182086656 | bytes 39092224 | tf_op jit(solution)/shard_map/bqkgc,bckd->bqkgd/dot_general | solution.py:54
  136.2 6.9 %all-to-all-start = ((bf16[1,128,32,128]{3,2,0,1:T(8,128)(2,1)}), bf16[1,128,32,128]{3,2,0,1:T(8,128)(2,1)S(1)}, u32[]{:S(2)}, u32[]{:S(2)}) async-start(bf16[1,128,32,128]{3,2,0,1:T(8,128)(2,1)} %bitcast.5), calls=%async_computation | async-start | bytes 2097152 | tf_op jit(solution)/shard_map/all_to_all | solution.py:68
  144.8 19.9 %all-to-all-done = bf16[1,128,32,128]{3,2,0,1:T(8,128)(2,1)S(1)} async-done(((bf16[1,128,32,128]{3,2,0,1:T(8,128)(2,1)}), bf16[1,128,32,128]{3,2,0,1:T(8,128)(2,1)S(1)}, u32[]{:S(2)}, u32[]{:S(2)}) %all-to-all-start) | async-done | bytes 1048608 | tf_op jit(solution)/shard_map/all_to_all | solution.py:68
  166.3 54.4 %all-gather.6.cloned.1.call-done = bf16[128,4096]{1,0:T(8,128)(2,1)} async-done(((bf16[8,4096]{1,0:T(8,128)(2,1)}), bf16[128,4096]{1,0:T(8,128)(2,1)}) %all-gather.6.cloned.1.call-update) | async-done | bytes 1048592 | tf_op jit(solution)/shard_map/all_gather | solution.py:79
  220.6 3.9 convolution_convert_fusion
  224.6 16.8 %all-reduce.3.cloned.1.call-done = bf16[128,512]{1,0:T(8,128)(2,1)} async-done(((bf16[128,512]{1,0:T(8,128)(2,1)}), bf16[128,512]{1,0:T(8,128)(2,1)}) %all-reduce.3.cloned.1.call-update) | async-done | bytes 131088 | tf_op jit(solution)/shard_map/psum | solution.py:83
  242.5 42.0 %psum.22 = f32[128]{0:T(128)S(1)} all-reduce(f32[128]{0:T(128)S(1)} %multiply_reduce_fusion), channel_id=1, replica_groups=mesh['groups'=1,'blk'=16,'head'=2] {'blk'}, use_global_device_ids=true, to_apply=%region_7.8 | all-reduce | flops 128 | bytes 1024 | tf_op jit(solution)/shard_map/psum | solution.py:85
  286.2 56.9 %all-gather.8.cloned.1.call-done = bf16[128,8192]{1,0:T(8,128)(2,1)} async-done(((bf16[128,512]{1,0:T(8,128)(2,1)}), bf16[128,8192]{1,0:T(8,128)(2,1)}) %all-gather.8.cloned.1.call-update) | async-done | bytes 2097168 | tf_op jit(solution)/shard_map/all_gather | solution.py:89
  343.1 5.3 %fusion.23 = f32[128,512]{1,0:T(8,128)S(1)} fusion(bf16[128,8192]{1,0:T(8,128)(2,1)} %all-gather.8.cloned.1.call-done, bf16[8192,512]{1,0:T(8,128)(2,1)} %param.17), kind=kOutput, calls=%fused_computation.53 | convolution fusion | flops 1073741824 | bytes 10747904 | tf_op jit(solution)/shard_map/dot_general | solution.py:90
  349.9 4.8 constant_dynamic-update-slice_fusion.15
  356.1 7.2 %collective-permute-done = bf16[128,512]{1,0:T(8,128)(2,1)S(1)} collective-permute-done((bf16[128,512]{1,0:T(8,128)(2,1)S(1)}, bf16[128,512]{1,0:T(8,128)(2,1)S(1)}, u32[]{:S(2)}, u32[]{:S(2)}) %collective-permute-start) | collective-permute-done | bytes 131104 | tf_op jit(solution)/shard_map/ppermute | solution.py:18
  363.3 8.6 %collective-permute-done.1 = bf16[128,512]{1,0:T(8,128)(2,1)S(1)} collective-permute-done((bf16[128,512]{1,0:T(8,128)(2,1)S(1)}, bf16[128,512]{1,0:T(8,128)(2,1)S(1)}, u32[]{:S(2)}, u32[]{:S(2)}) %collective-permute-start.1) | collective-permute-done | bytes 131104 | tf_op jit(solution)/shard_map/ppermute | solution.py:18
  371.9 8.6 %collective-permute-done.2 = bf16[128,512]{1,0:T(8,128)(2,1)S(1)} collective-permute-done((bf16[128,512]{1,0:T(8,128)(2,1)S(1)}, bf16[128,512]{1,0:T(8,128)(2,1)S(1)}, u32[]{:S(2)}, u32[]{:S(2)}) %collective-permute-start.2) | collective-permute-done | bytes 131104 | tf_op jit(solution)/shard_map/ppermute | solution.py:18
  380.5 9.1 %collective-permute-done.3 = bf16[128,512]{1,0:T(8,128)(2,1)S(1)} collective-permute-done((bf16[128,512]{1,0:T(8,128)(2,1)S(1)}, bf16[128,512]{1,0:T(8,128)(2,1)S(1)}, u32[]{:S(2)}, u32[]{:S(2)}) %collective-permute-start.3) | collective-permute-done | bytes 131104 | tf_op jit(solution)/shard_map/ppermute | solution.py:18
  389.6 9.7 %collective-permute-done.4 = bf16[128,512]{1,0:T(8,128)(2,1)S(1)} collective-permute-done((bf16[128,512]{1,0:T(8,128)(2,1)S(1)}, bf16[128,512]{1,0:T(8,128)(2,1)S(1)}, u32[]{:S(2)}, u32[]{:S(2)}) %collective-permute-start.4) | collective-permute-done | bytes 131104 | tf_op jit(solution)/shard_map/ppermute | solution.py:18
  399.2 8.8 %collective-permute-done.5 = bf16[128,512]{1,0:T(8,128)(2,1)S(1)} collective-permute-done((bf16[128,512]{1,0:T(8,128)(2,1)S(1)}, bf16[128,512]{1,0:T(8,128)(2,1)S(1)}, u32[]{:S(2)}, u32[]{:S(2)}) %collective-permute-start.5) | collective-permute-done | bytes 131104 | tf_op jit(solution)/shard_map/ppermute | solution.py:18
  408.1 8.6 %collective-permute-done.6 = bf16[128,512]{1,0:T(8,128)(2,1)S(1)} collective-permute-done((bf16[128,512]{1,0:T(8,128)(2,1)S(1)}, bf16[128,512]{1,0:T(8,128)(2,1)S(1)}, u32[]{:S(2)}, u32[]{:S(2)}) %collective-permute-start.6) | collective-permute-done | bytes 131104 | tf_op jit(solution)/shard_map/ppermute | solution.py:18
  416.6 8.6 %collective-permute-done.7 = bf16[128,512]{1,0:T(8,128)(2,1)S(1)} collective-permute-done((bf16[128,512]{1,0:T(8,128)(2,1)S(1)}, bf16[128,512]{1,0:T(8,128)(2,1)S(1)}, u32[]{:S(2)}, u32[]{:S(2)}) %collective-permute-start.7) | collective-permute-done | bytes 131104 | tf_op jit(solution)/shard_map/ppermute | solution.py:18
  425.3 8.5 %collective-permute-done.8 = bf16[128,512]{1,0:T(8,128)(2,1)S(1)} collective-permute-done((bf16[128,512]{1,0:T(8,128)(2,1)S(1)}, bf16[128,512]{1,0:T(8,128)(2,1)S(1)}, u32[]{:S(2)}, u32[]{:S(2)}) %collective-permute-start.8) | collective-permute-done | bytes 131104 | tf_op jit(solution)/shard_map/ppermute | solution.py:18
  433.8 8.5 %collective-permute-done.9 = bf16[128,512]{1,0:T(8,128)(2,1)S(1)} collective-permute-done((bf16[128,512]{1,0:T(8,128)(2,1)S(1)}, bf16[128,512]{1,0:T(8,128)(2,1)S(1)}, u32[]{:S(2)}, u32[]{:S(2)}) %collective-permute-start.9) | collective-permute-done | bytes 131104 | tf_op jit(solution)/shard_map/ppermute | solution.py:18
  442.4 9.1 %collective-permute-done.10 = bf16[128,512]{1,0:T(8,128)(2,1)S(1)} collective-permute-done((bf16[128,512]{1,0:T(8,128)(2,1)S(1)}, bf16[128,512]{1,0:T(8,128)(2,1)S(1)}, u32[]{:S(2)}, u32[]{:S(2)}) %collective-permute-start.10) | collective-permute-done | bytes 131104 | tf_op jit(solution)/shard_map/ppermute | solution.py:18
  451.5 9.6 %collective-permute-done.11 = bf16[128,512]{1,0:T(8,128)(2,1)S(1)} collective-permute-done((bf16[128,512]{1,0:T(8,128)(2,1)S(1)}, bf16[128,512]{1,0:T(8,128)(2,1)S(1)}, u32[]{:S(2)}, u32[]{:S(2)}) %collective-permute-start.11) | collective-permute-done | bytes 131104 | tf_op jit(solution)/shard_map/ppermute | solution.py:18
  461.2 8.7 %collective-permute-done.12 = bf16[128,512]{1,0:T(8,128)(2,1)S(1)} collective-permute-done((bf16[128,512]{1,0:T(8,128)(2,1)S(1)}, bf16[128,512]{1,0:T(8,128)(2,1)S(1)}, u32[]{:S(2)}, u32[]{:S(2)}) %collective-permute-start.12) | collective-permute-done | bytes 131104 | tf_op jit(solution)/shard_map/ppermute | solution.py:18
  470.0 8.5 %collective-permute-done.13 = bf16[128,512]{1,0:T(8,128)(2,1)S(1)} collective-permute-done((bf16[128,512]{1,0:T(8,128)(2,1)S(1)}, bf16[128,512]{1,0:T(8,128)(2,1)S(1)}, u32[]{:S(2)}, u32[]{:S(2)}) %collective-permute-start.13) | collective-permute-done | bytes 131104 | tf_op jit(solution)/shard_map/ppermute | solution.py:18
  478.5 8.5 %collective-permute-done.14 = bf16[128,512]{1,0:T(8,128)(2,1)S(1)} collective-permute-done((bf16[128,512]{1,0:T(8,128)(2,1)S(1)}, bf16[128,512]{1,0:T(8,128)(2,1)S(1)}, u32[]{:S(2)}, u32[]{:S(2)}) %collective-permute-start.14) | collective-permute-done | bytes 131104 | tf_op jit(solution)/shard_map/ppermute | solution.py:18
  487.1 5.3 %convolution_convert_fusion.1 = bf16[128,512]{1,0:T(8,128)(2,1)} fusion(bf16[128,8192]{1,0:T(8,128)(2,1)S(1)} %constant_dynamic-update-slice_fusion, bf16[8192,512]{1,0:T(8,128)(2,1)} %param.19), kind=kOutput, calls=%fused_computation.19 | convolution fusion | flops 1073807360 | bytes 10616832 | tf_op jit(solution)/shard_map/dot_general | solution.py:93
  492.4 13.9 %all-reduce.5.cloned.1.call-done = bf16[128,512]{1,0:T(8,128)(2,1)} async-done(((bf16[128,512]{1,0:T(8,128)(2,1)}), bf16[128,512]{1,0:T(8,128)(2,1)}) %all-reduce.5.cloned.1.call-update) | async-done | bytes 131088 | tf_op jit(solution)/shard_map/psum | solution.py:96
  (82 shorter events, 22.8 us)
Async XLA Ops:
  6.5 61.4 %all-gather.4.cloned.1.call-start = ((), (), s32[]{:S(2)}) async-start(), calls=%async_computation.3 | async-start | bytes 1114112 | tf_op jit(solution)/shard_map/all_gather | solution.py:43
  103.6 11.8 %all-to-all-start.1 = ((f32[16,1,256]{2,1,0:T(1,128)}), f32[16,1,256]{2,1,0:T(1,128)S(1)}, u32[]{:S(2)}, u32[]{:S(2)}) async-start(f32[16,1,256]{2,1,0:T(1,128)} %reshape.80), calls=%async_computation.1 | async-start | bytes 32768 | tf_op jit(solution)/shard_map/all_to_all | solution.py:66
  115.5 20.7 %all-to-all-start.2 = ((f32[16,1,256]{2,1,0:T(1,128)}), f32[16,1,256]{2,1,0:T(1,128)S(1)}, u32[]{:S(2)}, u32[]{:S(2)}) async-start(f32[16,1,256]{2,1,0:T(1,128)} %reshape.82), calls=%async_computation.2 | async-start | bytes 32768 | tf_op jit(solution)/shard_map/all_to_all | solution.py:65
  136.2 28.5 %all-to-all-start = ((bf16[1,128,32,128]{3,2,0,1:T(8,128)(2,1)}), bf16[1,128,32,128]{3,2,0,1:T(8,128)(2,1)S(1)}, u32[]{:S(2)}, u32[]{:S(2)}) async-start(bf16[1,128,32,128]{3,2,0,1:T(8,128)(2,1)} %bitcast.5), calls=%async_computation | async-start | bytes 2097152 | tf_op jit(solution)/shard_map/all_to_all | solution.py:68
  143.1 77.6 %all-gather.6.cloned.1.call-start = ((), (), s32[]{:S(2)}) async-start(), calls=%async_computation.4 | async-start | bytes 1114112 | tf_op jit(solution)/shard_map/all_gather | solution.py:79
  166.2 58.4 %copy-start.3 = (bf16[512]{0:T(512)(128)(2,1)S(1)}, bf16[512]{0:T(512)(128)(2,1)}, u32[]{:S(2)}) copy-start(bf16[512]{0:T(512)(128)(2,1)} %param.16) | copy-start | bytes 3076
  166.2 75.2 %copy-start.1 = (bf16[128,512]{1,0:T(8,128)(2,1)S(1)}, bf16[128,512]{1,0:T(8,128)(2,1)}, u32[]{:S(2)}) copy-start(bf16[128,512]{1,0:T(8,128)(2,1)} %param.14) | copy-start | bytes 393220
  166.2 75.2 %all-reduce.3.cloned.1.call-start = ((), (), s32[]{:S(2)}) async-start(), calls=%async_computation.5 | async-start | bytes 262144 | tf_op jit(solution)/shard_map/psum | solution.py:83
  224.5 118.5 %all-gather.8.cloned.1.call-start = ((), (), s32[]{:S(2)}) async-start(), calls=%async_computation.6 | async-start | bytes 2228224 | tf_op jit(solution)/shard_map/all_gather | solution.py:89
  286.2 220.2 %all-reduce.5.cloned.1.call-start = ((), (), s32[]{:S(2)}) async-start(), calls=%async_computation.7 | async-start | bytes 262144 | tf_op jit(solution)/shard_map/psum | solution.py:96
  348.3 1.6 copy-start
  354.7 8.6 %collective-permute-start = (bf16[128,512]{1,0:T(8,128)(2,1)S(1)}, bf16[128,512]{1,0:T(8,128)(2,1)S(1)}, u32[]{:S(2)}, u32[]{:S(2)}) collective-permute-start(bf16[128,512]{1,0:T(8,128)(2,1)S(1)} %get-tuple-element.10), channel_id=1, source_target_pairs={{0,2},{2,4},{4,6},{6,8},{8,10},{10,12},{12,14},{14,16},{16,18},{18... | collective-permute-start | bytes 393224 | tf_op jit(solution)/shard_map/ppermute | solution.py:18
  363.3 8.6 %collective-permute-start.1 = (bf16[128,512]{1,0:T(8,128)(2,1)S(1)}, bf16[128,512]{1,0:T(8,128)(2,1)S(1)}, u32[]{:S(2)}, u32[]{:S(2)}) collective-permute-start(bf16[128,512]{1,0:T(8,128)(2,1)S(1)} %collective-permute-done), channel_id=1, source_target_pairs={{0,2},{2,4},{4,6},{6,8},{8,10},{10,12},{12,14},{14,16},{16,18},{18... | collective-permute-start | bytes 393224 | tf_op jit(solution)/shard_map/ppermute | solution.py:18
  371.9 8.6 %collective-permute-start.2 = (bf16[128,512]{1,0:T(8,128)(2,1)S(1)}, bf16[128,512]{1,0:T(8,128)(2,1)S(1)}, u32[]{:S(2)}, u32[]{:S(2)}) collective-permute-start(bf16[128,512]{1,0:T(8,128)(2,1)S(1)} %collective-permute-done.1), channel_id=1, source_target_pairs={{0,2},{2,4},{4,6},{6,8},{8,10},{10,12},{12,14},{14,16},{16,18},{18... | collective-permute-start | bytes 393224 | tf_op jit(solution)/shard_map/ppermute | solution.py:18
  380.5 9.1 %collective-permute-start.3 = (bf16[128,512]{1,0:T(8,128)(2,1)S(1)}, bf16[128,512]{1,0:T(8,128)(2,1)S(1)}, u32[]{:S(2)}, u32[]{:S(2)}) collective-permute-start(bf16[128,512]{1,0:T(8,128)(2,1)S(1)} %collective-permute-done.2), channel_id=1, source_target_pairs={{0,2},{2,4},{4,6},{6,8},{8,10},{10,12},{12,14},{14,16},{16,18},{18... | collective-permute-start | bytes 393224 | tf_op jit(solution)/shard_map/ppermute | solution.py:18
  389.6 9.7 %collective-permute-start.4 = (bf16[128,512]{1,0:T(8,128)(2,1)S(1)}, bf16[128,512]{1,0:T(8,128)(2,1)S(1)}, u32[]{:S(2)}, u32[]{:S(2)}) collective-permute-start(bf16[128,512]{1,0:T(8,128)(2,1)S(1)} %collective-permute-done.3), channel_id=1, source_target_pairs={{0,2},{2,4},{4,6},{6,8},{8,10},{10,12},{12,14},{14,16},{16,18},{18... | collective-permute-start | bytes 393224 | tf_op jit(solution)/shard_map/ppermute | solution.py:18
  399.2 8.8 %collective-permute-start.5 = (bf16[128,512]{1,0:T(8,128)(2,1)S(1)}, bf16[128,512]{1,0:T(8,128)(2,1)S(1)}, u32[]{:S(2)}, u32[]{:S(2)}) collective-permute-start(bf16[128,512]{1,0:T(8,128)(2,1)S(1)} %collective-permute-done.4), channel_id=1, source_target_pairs={{0,2},{2,4},{4,6},{6,8},{8,10},{10,12},{12,14},{14,16},{16,18},{18... | collective-permute-start | bytes 393224 | tf_op jit(solution)/shard_map/ppermute | solution.py:18
  408.1 8.6 %collective-permute-start.6 = (bf16[128,512]{1,0:T(8,128)(2,1)S(1)}, bf16[128,512]{1,0:T(8,128)(2,1)S(1)}, u32[]{:S(2)}, u32[]{:S(2)}) collective-permute-start(bf16[128,512]{1,0:T(8,128)(2,1)S(1)} %collective-permute-done.5), channel_id=1, source_target_pairs={{0,2},{2,4},{4,6},{6,8},{8,10},{10,12},{12,14},{14,16},{16,18},{18... | collective-permute-start | bytes 393224 | tf_op jit(solution)/shard_map/ppermute | solution.py:18
  416.6 8.6 %collective-permute-start.7 = (bf16[128,512]{1,0:T(8,128)(2,1)S(1)}, bf16[128,512]{1,0:T(8,128)(2,1)S(1)}, u32[]{:S(2)}, u32[]{:S(2)}) collective-permute-start(bf16[128,512]{1,0:T(8,128)(2,1)S(1)} %collective-permute-done.6), channel_id=1, source_target_pairs={{0,2},{2,4},{4,6},{6,8},{8,10},{10,12},{12,14},{14,16},{16,18},{18... | collective-permute-start | bytes 393224 | tf_op jit(solution)/shard_map/ppermute | solution.py:18
  425.2 8.6 %collective-permute-start.8 = (bf16[128,512]{1,0:T(8,128)(2,1)S(1)}, bf16[128,512]{1,0:T(8,128)(2,1)S(1)}, u32[]{:S(2)}, u32[]{:S(2)}) collective-permute-start(bf16[128,512]{1,0:T(8,128)(2,1)S(1)} %collective-permute-done.7), channel_id=1, source_target_pairs={{0,2},{2,4},{4,6},{6,8},{8,10},{10,12},{12,14},{14,16},{16,18},{18... | collective-permute-start | bytes 393224 | tf_op jit(solution)/shard_map/ppermute | solution.py:18
  433.8 8.6 %collective-permute-start.9 = (bf16[128,512]{1,0:T(8,128)(2,1)S(1)}, bf16[128,512]{1,0:T(8,128)(2,1)S(1)}, u32[]{:S(2)}, u32[]{:S(2)}) collective-permute-start(bf16[128,512]{1,0:T(8,128)(2,1)S(1)} %collective-permute-done.8), channel_id=1, source_target_pairs={{0,2},{2,4},{4,6},{6,8},{8,10},{10,12},{12,14},{14,16},{16,18},{18... | collective-permute-start | bytes 393224 | tf_op jit(solution)/shard_map/ppermute | solution.py:18
  442.3 9.1 %collective-permute-start.10 = (bf16[128,512]{1,0:T(8,128)(2,1)S(1)}, bf16[128,512]{1,0:T(8,128)(2,1)S(1)}, u32[]{:S(2)}, u32[]{:S(2)}) collective-permute-start(bf16[128,512]{1,0:T(8,128)(2,1)S(1)} %collective-permute-done.9), channel_id=1, source_target_pairs={{0,2},{2,4},{4,6},{6,8},{8,10},{10,12},{12,14},{14,16},{16,18},{18... | collective-permute-start | bytes 393224 | tf_op jit(solution)/shard_map/ppermute | solution.py:18
  451.5 9.6 %collective-permute-start.11 = (bf16[128,512]{1,0:T(8,128)(2,1)S(1)}, bf16[128,512]{1,0:T(8,128)(2,1)S(1)}, u32[]{:S(2)}, u32[]{:S(2)}) collective-permute-start(bf16[128,512]{1,0:T(8,128)(2,1)S(1)} %collective-permute-done.10), channel_id=1, source_target_pairs={{0,2},{2,4},{4,6},{6,8},{8,10},{10,12},{12,14},{14,16},{16,18},{18... | collective-permute-start | bytes 393224 | tf_op jit(solution)/shard_map/ppermute | solution.py:18
  461.1 8.8 %collective-permute-start.12 = (bf16[128,512]{1,0:T(8,128)(2,1)S(1)}, bf16[128,512]{1,0:T(8,128)(2,1)S(1)}, u32[]{:S(2)}, u32[]{:S(2)}) collective-permute-start(bf16[128,512]{1,0:T(8,128)(2,1)S(1)} %collective-permute-done.11), channel_id=1, source_target_pairs={{0,2},{2,4},{4,6},{6,8},{8,10},{10,12},{12,14},{14,16},{16,18},{18... | collective-permute-start | bytes 393224 | tf_op jit(solution)/shard_map/ppermute | solution.py:18
  469.9 8.6 %collective-permute-start.13 = (bf16[128,512]{1,0:T(8,128)(2,1)S(1)}, bf16[128,512]{1,0:T(8,128)(2,1)S(1)}, u32[]{:S(2)}, u32[]{:S(2)}) collective-permute-start(bf16[128,512]{1,0:T(8,128)(2,1)S(1)} %collective-permute-done.12), channel_id=1, source_target_pairs={{0,2},{2,4},{4,6},{6,8},{8,10},{10,12},{12,14},{14,16},{16,18},{18... | collective-permute-start | bytes 393224 | tf_op jit(solution)/shard_map/ppermute | solution.py:18
  478.5 8.6 %collective-permute-start.14 = (bf16[128,512]{1,0:T(8,128)(2,1)S(1)}, bf16[128,512]{1,0:T(8,128)(2,1)S(1)}, u32[]{:S(2)}, u32[]{:S(2)}) collective-permute-start(bf16[128,512]{1,0:T(8,128)(2,1)S(1)} %collective-permute-done.13), channel_id=1, source_target_pairs={{0,2},{2,4},{4,6},{6,8},{8,10},{10,12},{12,14},{14,16},{16,18},{18... | collective-permute-start | bytes 393224 | tf_op jit(solution)/shard_map/ppermute | solution.py:18
  487.1 19.3 %copy-start.2 = (bf16[128,512]{1,0:T(8,128)(2,1)S(1)}, bf16[128,512]{1,0:T(8,128)(2,1)}, u32[]{:S(2)}) copy-start(bf16[128,512]{1,0:T(8,128)(2,1)} %all-reduce.3.cloned.1.call-done) | copy-start | bytes 393220
Sparse Core Ops, SparseCore 0:
  10.1 57.7 all-gather.3
  166.3 54.2 all-gather.5
  224.7 16.7 all-reduce.2
  286.3 56.7 all-gather.7
  492.6 13.7 all-reduce.4
